TPU v7x, 256 devices: a whole 4x4x8 slice. The times are simulated.
256 devices in a mesh: grp: 4 (over y), col: 64 (over x, z, core).
Axes of the slice: x: 4, y: 4, z: 8, core: 2. Of those that a mesh axis runs over, the one named last changes fastest.
Arguments:
- panels: bfloat16 [256, 4, 512, 512], P('col', None, 'grp'), may hold values from -1.296875 to 1.296875
- parent: float32 [256, 512, 512], P('col', 'grp'), may hold values from -6 to 6
- src_block: int32 [64, 40], P('col'), may hold values from 0 to 39, each once within a row
- dest_owner: int32 [2560, 1], P('col'), may hold values from 0 to 63; in each aligned block of 40 rows (0 to 39, 40 to 79, ...) no two rows name the same one
- target: int32 [2560], P('col'), may hold values from 0 to 3
- counts: int32 [64], P('col'), may hold values from 20 to 40, as said below
Outputs:
- assembled: float32 [256, 512, 512], P('col', 'grp')
Inputs may be any that keep to these rules, and one draw needn't show every extreme that they name: `src_block`: each row of a column rank is a permutation of the 40 block pairs. `dest_owner`: among the 40 slots of one column rank at most 1 name the same owner. The live slots of a rank are its first counts[c]; some rank has all 40 live.
All inputs are finite; a program needn't handle non-finite values.
Results may differ from a plain program's by a relative error of at most 0.0026.
Values may be sent and summed in bfloat16 or wider, within the bound.
A program may use at most 128 MiB of HBM per device.

v0:
```python
import jax
import jax.numpy as jnp
import numpy as np
from jax import lax
from jax.sharding import PartitionSpec as P


def place_slots(src_block, dest_owner, target, counts, peer_count, capacity):
    slot_count = src_block.shape[1]
    slot_index = jnp.arange(slot_count, dtype=jnp.int32)
    owner_rank = dest_owner[:, 0]
    matches = (owner_rank[:, None] == jnp.arange(peer_count, dtype=jnp.int32)[None, :]).astype(
        jnp.int32
    )
    earlier = jnp.cumsum(matches, axis=0) - matches
    rank_in = jnp.sum(earlier * matches, axis=1)
    position = owner_rank * capacity + rank_in
    is_live = slot_index < counts[0]
    routed = jnp.zeros((peer_count * capacity,), jnp.int32).at[position].set(target)
    return (src_block[0], position, is_live, routed.reshape(peer_count, capacity))


def pack_updates(flat_updates, chosen, position, is_live, peer_count, capacity):
    picked = flat_updates[chosen]
    picked = jnp.where(is_live[:, None, None], picked, jnp.zeros_like(picked))
    buffer = (
        jnp.zeros((peer_count * capacity,) + picked.shape[1:], picked.dtype)
        .at[position]
        .set(picked)
    )
    return buffer.reshape((peer_count, capacity) + picked.shape[1:])


def assemble(received, labels, targets):
    arrived = received.reshape((-1,) + received.shape[2:])
    flat_labels = labels.reshape(-1)
    select = (flat_labels[None, :] == jnp.arange(targets, dtype=jnp.int32)[:, None]).astype(
        jnp.bfloat16
    )
    return jnp.einsum("tn,nrc->trc", select, arrived, preferred_element_type=jnp.float32)


def pair_products(own_rows, piece_rows):
    blocks = own_rows.shape[1]
    upper_table = np.array([a for a in range(blocks) for b in range(a + 1)], np.int32)
    lower_table = np.array([b for a in range(blocks) for b in range(a + 1)], np.int32)
    left_rows = own_rows[:, upper_table]
    right_rows = piece_rows[:, lower_table]
    return jnp.einsum(
        "fprw,fpcw->fprc", left_rows, right_rows, preferred_element_type=jnp.float32
    ).astype(jnp.bfloat16)


def per_device(panels, parent, src_block, dest_owner, target, counts):
    fronts, blocks, quarter, _ = panels.shape
    pair_count = blocks * (blocks + 1) // 2
    peer_count = lax.axis_size("col")
    slot_count = src_block.shape[1]
    capacity = (slot_count + peer_count - 1) // peer_count + slot_count // (2 * peer_count)
    targets = parent.shape[0]
    chosen, position, is_live, routed = place_slots(
        src_block, dest_owner, target, counts, peer_count, capacity
    )
    products = pair_products(panels, lax.all_gather(panels, "grp", axis=2, tiled=True))
    flat_updates = products.reshape(fronts * pair_count, quarter, products.shape[3])
    buffer = pack_updates(flat_updates, chosen, position, is_live, peer_count, capacity)
    received, labels = (
        lax.all_to_all(buffer, "col", split_axis=0, concat_axis=0, tiled=True),
        lax.all_to_all(routed, "col", split_axis=0, concat_axis=0, tiled=True),
    )
    return parent - assemble(received, labels, targets)


def solution(mesh):
    placed = (
        P("col", None, "grp", None),
        P("col", "grp", None),
        P("col", None),
        P("col", None),
        P("col"),
        P("col"),
    )
    return jax.shard_map(
        per_device, mesh=mesh, in_specs=placed, out_specs=P("col", "grp", None), check_vma=False
    )
```

profile of v0, /device:TPU:1, one launch (start us, length us, event | category | flops | bytes accessed | tf_op | source)
XLA Modules:
  0.0 390.6 jit_solution(11302547754613624316)
XLA Ops:
  6.5 0.0 copy-start.1
  6.5 0.0 copy-start.2
  6.5 0.0 all-gather.2.cloned.1.call-start
  6.5 0.7 all-gather.2.cloned.1.call-update
  7.3 0.7 fusion.13
  8.0 0.1 reduce_window_sum.11
  8.1 0.8 select_reduce_fusion
  8.9 0.7 fusion.17
  9.6 0.8 scatter_custom_fusion
  10.4 0.7 copy.36
  11.1 13.0 %all-to-all-start = ((s32[64,1,1]{2,1,0:T(1,128)}), s32[64,1,1]{2,1,0:T(1,128)S(1)}, u32[]{:S(2)}, u32[]{:S(2)}) async-start(s32[64,1,1]{2,1,0:T(1,128)} %copy.36), calls=%async_computation | async-start | bytes 65536 | tf_op jit(solution)/shard_map/all_to_all | solution.py:69
  24.1 0.7 pad_clamp_fusion.2
  24.8 5.7 %gather_fusion = bf16[10,4,128,512]{3,2,1,0:T(8,128)(2,1)} fusion(bf16[4,4,128,512]{3,2,1,0:T(8,128)(2,1)} %param.10, s32[1024]{0:T(1024)S(1)} %pad_clamp_fusion.2), kind=kCustom, calls=%fused_computation | custom fusion | bytes 10485800 | tf_op jit(solution)/shard_map/gather | solution.py:47
  31.1 0.0 copy-done.1
  31.1 0.0 copy-done.2
  31.2 67.3 %all-gather.2.cloned.1.call-done = bf16[4,4,512,512]{3,2,1,0:T(8,128)(2,1)} async-done(((bf16[4,4,128,512]{3,2,1,0:T(8,128)(2,1)}), bf16[4,4,512,512]{3,2,1,0:T(8,128)(2,1)}) %all-gather.2.cloned.1.call-update) | async-done | bytes 8388624 | tf_op jit(solution)/shard_map/all_gather | solution.py:64
  98.4 6.0 %fusion.22 = (bf16[4,4,256,512]{3,2,1,0:T(8,128)(2,1)}, bf16[4,4,256,512]{3,2,1,0:T(8,128)(2,1)}) fusion(bf16[4,4,512,512]{3,2,1,0:T(8,128)(2,1)} %all-gather.2.cloned.1.call-done), kind=kLoop, calls=%fused_computation.37 | loop fusion | bytes 16777216 | tf_op jit(solution)/shard_map/gather | solution.py:48
  104.5 7.6 %gather_fusion.2 = bf16[10,4,256,512]{3,2,1,0:T(8,128)(2,1)} fusion(bf16[4,4,256,512]{3,2,1,0:T(8,128)(2,1)} %get-tuple-element.5, s32[1024]{0:T(1024)S(1)} %pad_clamp_fusion.1), kind=kCustom, calls=%fused_computation.2 | custom fusion | bytes 20971560 | tf_op jit(solution)/shard_map/gather | solution.py:48
  112.1 0.0 slice-start
  112.1 7.7 %gather_fusion.3 = bf16[10,4,256,512]{3,2,1,0:T(8,128)(2,1)} fusion(bf16[4,4,256,512]{3,2,1,0:T(8,128)(2,1)} %get-tuple-element.6, s32[1024]{0:T(1024)S(1)} %pad_clamp_fusion.1), kind=kCustom, calls=%fused_computation.3 | custom fusion | bytes 20971560 | tf_op jit(solution)/shard_map/gather | solution.py:48
  119.7 0.0 slice-start.1
  119.7 12.3 %copy_bitcast_fusion = (bf16[4,10,256,512]{3,2,1,0:T(8,128)(2,1)S(1)}, bf16[4,10,256,512]{3,2,1,0:T(8,128)(2,1)}) fusion(bf16[10,4,256,512]{3,2,1,0:T(8,128)(2,1)} %gather_fusion.3, bf16[10,4,256,512]{3,2,1,0:T(8,128)(2,1)} %gather_fusion.2), kind=kLoop, calls=%fused_computation.10 | loop fusion | bytes 41943040 | tf_op jit(solution)/shard_map/gather | solution.py:48
  132.1 0.0 slice-done
  132.1 0.0 slice-done.1
  132.1 10.5 %fusion.8 = bf16[4,10,128,512]{3,2,1,0:T(8,128)(2,1)} fusion(bf16[4,10,256,512]{3,2,1,0:T(8,128)(2,1)S(1)} %get-tuple-element.7, bf16[4,10,256,512]{3,2,1,0:T(8,128)(2,1)} %get-tuple-element.8, bf16[10,4,128,512]{3,2,1,0:T(8,128)(2,1)S(1)} %bitcast.34), kind=kOutput, calls=%fused_computation.17 | convolution fusion | flops 2728919040 | bytes 31457280 | tf_op jit(solution)/shard_map/fprw,fpcw->fprc/dot_general | solution.py:49
  142.6 7.2 %gather_fusion.1 = bf16[40,128,512]{2,1,0:T(8,128)(2,1)} fusion(bf16[40,128,512]{2,1,0:T(8,128)(2,1)} %bitcast.35, s32[1024]{0:T(1024)S(1)} %pad_clamp_fusion), kind=kCustom, calls=%fused_computation.1 | custom fusion | bytes 10485920 | tf_op jit(solution)/shard_map/gather | solution.py:24
  149.8 5.3 %broadcast_select_fusion = bf16[40,128,512]{2,1,0:T(8,128)(2,1)} fusion(bf16[40,128,512]{2,1,0:T(8,128)(2,1)} %gather_fusion.1, pred[40]{0:T(512)(128)(4,1)S(1)} %iota_compare_fusion.2), kind=kLoop, calls=%fused_computation.16 | loop fusion | flops 2621440 | bytes 10485800 | tf_op jit(solution)/shard_map/jit(_where)/select_n | solution.py:25
  155.1 4.2 %broadcast_in_dim.30 = bf16[64,128,512]{2,1,0:T(8,128)(2,1)} broadcast(bf16[]{:T(256)} %constant.10.clone.1), dimensions={} | broadcast | bytes 8388610 | tf_op jit(solution)/shard_map/broadcast_in_dim | solution.py:27
  159.3 14.1 %scatter_fusion = bf16[64,128,512]{2,1,0:T(8,128)(2,1)} fusion(bf16[64,128,512]{2,1,0:T(8,128)(2,1)} %broadcast_in_dim.30, s32[40]{0:T(128)S(1)} %fusion.17, bf16[40,128,512]{2,1,0:T(8,128)(2,1)} %broadcast_select_fusion), kind=kCustom, calls=%fused_computation.5 | custom fusion | bytes 15728800 | tf_op jit(solution)/shard_map/scatter | solution.py:29
  173.4 0.0 all-to-all-done
  173.4 11.0 %all-to-all-start.1 = ((bf16[64,1,128,512]{3,2,1,0:T(8,128)(2,1)}), bf16[64,1,128,512]{3,2,1,0:T(8,128)(2,1)}, u32[]{:S(2)}, u32[]{:S(2)}) async-start(bf16[64,1,128,512]{3,2,1,0:T(8,128)(2,1)} %bitcast.32), calls=%async_computation.1 | async-start | bytes 16777216 | tf_op jit(solution)/shard_map/all_to_all | solution.py:68
  184.3 0.0 copy-start
  184.4 1.2 reduce
  185.6 184.5 %all-to-all-done.1 = bf16[64,1,128,512]{3,2,1,0:T(8,128)(2,1)} async-done(((bf16[64,1,128,512]{3,2,1,0:T(8,128)(2,1)}), bf16[64,1,128,512]{3,2,1,0:T(8,128)(2,1)}, u32[]{:S(2)}, u32[]{:S(2)}) %all-to-all-start.1) | async-done | bytes 8388640 | tf_op jit(solution)/shard_map/all_to_all | solution.py:68
  370.1 12.3 %fusion.4 = f32[4,128,512]{2,0,1:T(4,128)S(1)} fusion(bf16[64,1,128,512]{3,2,1,0:T(8,128)(2,1)} %all-to-all-done.1, s32[64]{0:T(128)S(1)} %reduce), kind=kOutput, calls=%fused_computation.12 | convolution fusion | flops 33554688 | bytes 9437440 | tf_op jit(solution)/shard_map/tn,nrc->trc/dot_general | solution.py:40
  382.3 0.0 copy-done
  382.3 1.4 copy_subtract_fusion
  (5 shorter events, 0.0 us)
Async XLA Ops:
  6.5 24.6 %copy-start.1 = (s32[10]{0:T(128)S(1)}, s32[10]{0:T(128)}, u32[]{:S(2)}) copy-start(s32[10]{0:T(128)} %constant.35) | copy-start | bytes 124
  6.5 24.6 %copy-start.2 = (s32[1,40]{1,0:T(1,128)S(1)}, s32[1,40]{1,0:T(1,128)}, u32[]{:S(2)}) copy-start(s32[1,40]{1,0:T(1,128)} %param.12) | copy-start | bytes 484
  6.5 91.9 %all-gather.2.cloned.1.call-start = ((), (), s32[]{:S(2)}) async-start(), calls=%async_computation.2 | async-start | bytes 10485760 | tf_op jit(solution)/shard_map/all_gather | solution.py:64
  11.1 162.3 %all-to-all-start = ((s32[64,1,1]{2,1,0:T(1,128)}), s32[64,1,1]{2,1,0:T(1,128)S(1)}, u32[]{:S(2)}, u32[]{:S(2)}) async-start(s32[64,1,1]{2,1,0:T(1,128)} %copy.36), calls=%async_computation | async-start | bytes 65536 | tf_op jit(solution)/shard_map/all_to_all | solution.py:69
  112.1 20.0 %slice-start = ((s8[5242880]{0:T(1024)(128)(4,1)}), s8[1048576]{0:T(1024)(128)(4,1)S(1)}, s32[]{:S(2)}) async-start(s8[5242880]{0:T(1024)(128)(4,1)} %bitcast.33), calls=%async_computation.3 | async-start | bytes 2097152
  119.7 12.4 %slice-start.1 = ((s8[5242880]{0:T(1024)(128)(4,1)}), s8[4194304]{0:T(1024)(128)(4,1)S(1)}, s32[]{:S(2)}) async-start(s8[5242880]{0:T(1024)(128)(4,1)} %bitcast.33), calls=%async_computation.4 | async-start | bytes 8388608
  173.4 196.7 %all-to-all-start.1 = ((bf16[64,1,128,512]{3,2,1,0:T(8,128)(2,1)}), bf16[64,1,128,512]{3,2,1,0:T(8,128)(2,1)}, u32[]{:S(2)}, u32[]{:S(2)}) async-start(bf16[64,1,128,512]{3,2,1,0:T(8,128)(2,1)} %bitcast.32), calls=%async_computation.1 | async-start | bytes 16777216 | tf_op jit(solution)/shard_map/all_to_all | solution.py:68
  184.3 198.0 %copy-start = (f32[4,128,512]{2,1,0:T(8,128)S(1)}, f32[4,128,512]{2,1,0:T(8,128)}, u32[]{:S(2)}) copy-start(f32[4,128,512]{2,1,0:T(8,128)} %param.11) | copy-start | bytes 3145732
Sparse Core Ops, SparseCore 0:
  9.1 89.2 all-gather.1
where the time goes:
time: 391 us
  waiting for transfers between devices  252 us (64%)
  local copies, waits for them, and re-layouts  66.4 us (17%)
  starting transfers between devices  23.9 us (6%)
  matrix products  22.8 us (6%)
  between operations  14.1 us (4%)
  other arithmetic  10.9 us (3%)
    all_to_all x1, waiting for transfers between devices, per_device(): lax.all_to_all(buffer, 'col', split_axis=0, concat_axis=0, tiled=True)  184 us
    all_gather x1, waiting for transfers between devices, per_device(): lax.all_gather(panels, 'grp', axis=2, tiled=True)  67.3 us
    gather x4, local copies, waits for them, and re-layouts, pair_products(): right_rows = piece_rows[:, lower_table]  33.6 us
    scatter x1, local copies, waits for them, and re-layouts, pack_updates(): buffer = jnp.zeros((peer_count * capacity,) + picked.shape[1:], picked.dt...  14.1 us
    all_to_all x1, starting transfers between devices, per_device(): lax.all_to_all(routed, 'col', split_axis=0, concat_axis=0, tiled=True)  13 us
    dot_general x1, matrix products, assemble(): jnp.einsum('tn,nrc->trc', select, arrived, preferred_element_type=jnp.flo...  12.3 us
    all_to_all x1, starting transfers between devices, per_device(): lax.all_to_all(buffer, 'col', split_axis=0, concat_axis=0, tiled=True)  11 us
    dot_general x1, matrix products, pair_products(): jnp.einsum('fprw,fpcw->fprc', left_rows, right_rows, preferred_element_ty...  10.5 us
  transfers between devices with their start and end apart: 3, of which 2 were waited for; matrix products, arithmetic and copies ran while one was open for 22% of the time, Pallas kernels for 0%

commit v1 on v0

--- a/solution.py
+++ b/solution.py
@@ -61,7 +61,7 @@
     chosen, position, is_live, routed = place_slots(
         src_block, dest_owner, target, counts, peer_count, capacity
     )
-    products = pair_products(panels, lax.all_gather(panels, "grp", axis=2, tiled=True))
+    products = pair_products(panels, jnp.concatenate(lax.all_gather(panels, "grp"), axis=2))
     flat_updates = products.reshape(fronts * pair_count, quarter, products.shape[3])
     buffer = pack_updates(flat_updates, chosen, position, is_live, peer_count, capacity)
     received, labels = (

time: 391 us -> 399 us (1.020)
  local copies, waits for them, and re-layouts: 66.4 us -> 73.8 us
    reshape x0 -> x1, local copies, waits for them, and re-layouts: none -> 7.6 us  [per_device(): jnp.concatenate(lax.all_gather(panels, 'grp'), axis=2)]
  transfers between devices with their start and end apart: 3 -> 3, of which waited for: 2 -> 2; matrix products, arithmetic and copies ran while one was open for 22% -> 24% of each run, Pallas kernels for 0% -> 0%
where the time goes in v1:
time: 399 us; the launch traced here: 398 us
  waiting for transfers between devices  252 us (63%)
  local copies, waits for them, and re-layouts  73.8 us (18%)
  starting transfers between devices  24 us (6%)
  matrix products  22.8 us (6%)
  between operations  14.1 us (4%)
  other arithmetic  10.9 us (3%)
    all_to_all x1, waiting for transfers between devices, per_device(): lax.all_to_all(buffer, 'col', split_axis=0, concat_axis=0, tiled=True)  184 us
    all_gather x1, waiting for transfers between devices, per_device(): lax.all_gather(panels, 'grp')  67.3 us
    gather x4, local copies, waits for them, and re-layouts, pair_products(): right_rows = piece_rows[:, lower_table]  33.4 us
    scatter x1, local copies, waits for them, and re-layouts, pack_updates(): buffer = jnp.zeros((peer_count * capacity,) + picked.shape[1:], picked.dt...  14.1 us
    all_to_all x1, starting transfers between devices, per_device(): lax.all_to_all(routed, 'col', split_axis=0, concat_axis=0, tiled=True)  13 us
    dot_general x1, matrix products, assemble(): jnp.einsum('tn,nrc->trc', select, arrived, preferred_element_type=jnp.flo...  12.3 us
    all_to_all x1, starting transfers between devices, per_device(): lax.all_to_all(buffer, 'col', split_axis=0, concat_axis=0, tiled=True)  11 us
    dot_general x1, matrix products, pair_products(): jnp.einsum('fprw,fpcw->fprc', left_rows, right_rows, preferred_element_ty...  10.5 us
  transfers between devices with their start and end apart: 3, of which 2 were waited for; matrix products, arithmetic and copies ran while one was open for 24% of the time, Pallas kernels for 0%

profile of v1, /device:TPU:1, one launch (start us, length us, event | category | flops | bytes accessed | tf_op | source)
XLA Modules:
  0.0 398.0 jit_solution(4954429753130246199)
XLA Ops:
  6.5 0.0 copy-start.1
  6.5 0.0 copy-start.2
  6.5 0.0 all-gather.3.cloned.1.call-start
  6.5 0.7 all-gather.3.cloned.1.call-update
  7.3 0.7 fusion.13
  8.0 0.1 reduce_window_sum.11
  8.1 0.8 select_reduce_fusion
  8.9 0.7 fusion.17
  9.6 0.8 scatter_custom_fusion
  10.4 0.7 copy.45
  11.1 13.0 %all-to-all-start = ((s32[64,1,1]{2,1,0:T(1,128)}), s32[64,1,1]{2,1,0:T(1,128)S(1)}, u32[]{:S(2)}, u32[]{:S(2)}) async-start(s32[64,1,1]{2,1,0:T(1,128)} %copy.45), calls=%async_computation | async-start | bytes 65536 | tf_op jit(solution)/shard_map/all_to_all | solution.py:69
  24.1 0.7 pad_clamp_fusion.2
  24.8 5.7 %gather_fusion = bf16[10,4,128,512]{3,2,1,0:T(8,128)(2,1)} fusion(bf16[4,4,128,512]{3,2,1,0:T(8,128)(2,1)} %param.10, s32[1024]{0:T(1024)S(1)} %pad_clamp_fusion.2), kind=kCustom, calls=%fused_computation | custom fusion | bytes 10485800 | tf_op jit(solution)/shard_map/gather | solution.py:47
  31.1 0.0 copy-done.1
  31.1 0.0 copy-done.2
  31.2 67.3 %all-gather.3.cloned.1.call-done = bf16[16,4,128,512]{3,2,1,0:T(8,128)(2,1)} async-done(((bf16[4,4,128,512]{3,2,1,0:T(8,128)(2,1)}), bf16[16,4,128,512]{3,2,1,0:T(8,128)(2,1)}) %all-gather.3.cloned.1.call-update) | async-done | bytes 8388624 | tf_op jit(solution)/shard_map/all_gather | solution.py:64
  98.4 7.6 %copy.46 = bf16[4,4,4,128,512]{4,3,2,1,0:T(8,128)(2,1)} copy(bf16[4,4,4,128,512]{4,3,1,0,2:T(8,128)(2,1)} %bitcast.38) | data formatting | bytes 16777216 | tf_op jit(solution)/shard_map/reshape | solution.py:64
  106.0 5.8 %fusion.22 = (bf16[4,4,256,512]{3,2,1,0:T(8,128)(2,1)}, bf16[4,4,256,512]{3,2,1,0:T(8,128)(2,1)}) fusion(bf16[4,4,512,512]{3,2,1,0:T(8,128)(2,1)} %bitcast.37), kind=kLoop, calls=%fused_computation.37 | loop fusion | bytes 16777216 | tf_op jit(solution)/shard_map/gather | solution.py:48
  111.8 7.6 %gather_fusion.2 = bf16[10,4,256,512]{3,2,1,0:T(8,128)(2,1)} fusion(bf16[4,4,256,512]{3,2,1,0:T(8,128)(2,1)} %get-tuple-element.5, s32[1024]{0:T(1024)S(1)} %pad_clamp_fusion.1), kind=kCustom, calls=%fused_computation.2 | custom fusion | bytes 20971560 | tf_op jit(solution)/shard_map/gather | solution.py:48
  119.5 0.0 slice-start
  119.5 7.7 %gather_fusion.3 = bf16[10,4,256,512]{3,2,1,0:T(8,128)(2,1)} fusion(bf16[4,4,256,512]{3,2,1,0:T(8,128)(2,1)} %get-tuple-element.6, s32[1024]{0:T(1024)S(1)} %pad_clamp_fusion.1), kind=kCustom, calls=%fused_computation.3 | custom fusion | bytes 20971560 | tf_op jit(solution)/shard_map/gather | solution.py:48
  127.1 0.0 slice-start.1
  127.1 12.3 %copy_bitcast_fusion = (bf16[4,10,256,512]{3,2,1,0:T(8,128)(2,1)S(1)}, bf16[4,10,256,512]{3,2,1,0:T(8,128)(2,1)}) fusion(bf16[10,4,256,512]{3,2,1,0:T(8,128)(2,1)} %gather_fusion.3, bf16[10,4,256,512]{3,2,1,0:T(8,128)(2,1)} %gather_fusion.2), kind=kLoop, calls=%fused_computation.10 | loop fusion | bytes 41943040 | tf_op jit(solution)/shard_map/gather | solution.py:48
  139.5 0.0 slice-done
  139.5 0.0 slice-done.1
  139.5 10.5 %fusion.8 = bf16[4,10,128,512]{3,2,1,0:T(8,128)(2,1)} fusion(bf16[4,10,256,512]{3,2,1,0:T(8,128)(2,1)S(1)} %get-tuple-element.7, bf16[4,10,256,512]{3,2,1,0:T(8,128)(2,1)} %get-tuple-element.8, bf16[10,4,128,512]{3,2,1,0:T(8,128)(2,1)S(1)} %bitcast.40), kind=kOutput, calls=%fused_computation.17 | convolution fusion | flops 2728919040 | bytes 31457280 | tf_op jit(solution)/shard_map/fprw,fpcw->fprc/dot_general | solution.py:49
  150.0 7.2 %gather_fusion.1 = bf16[40,128,512]{2,1,0:T(8,128)(2,1)} fusion(bf16[40,128,512]{2,1,0:T(8,128)(2,1)} %bitcast.41, s32[1024]{0:T(1024)S(1)} %pad_clamp_fusion), kind=kCustom, calls=%fused_computation.1 | custom fusion | bytes 10485920 | tf_op jit(solution)/shard_map/gather | solution.py:24
  157.2 5.3 %broadcast_select_fusion = bf16[40,128,512]{2,1,0:T(8,128)(2,1)} fusion(bf16[40,128,512]{2,1,0:T(8,128)(2,1)} %gather_fusion.1, pred[40]{0:T(512)(128)(4,1)S(1)} %iota_compare_fusion.2), kind=kLoop, calls=%fused_computation.16 | loop fusion | flops 2621440 | bytes 10485800 | tf_op jit(solution)/shard_map/jit(_where)/select_n | solution.py:25
  162.4 4.2 %broadcast_in_dim.30 = bf16[64,128,512]{2,1,0:T(8,128)(2,1)} broadcast(bf16[]{:T(256)} %constant.10.clone.1), dimensions={} | broadcast | bytes 8388610 | tf_op jit(solution)/shard_map/broadcast_in_dim | solution.py:27
  166.7 14.1 %scatter_fusion = bf16[64,128,512]{2,1,0:T(8,128)(2,1)} fusion(bf16[64,128,512]{2,1,0:T(8,128)(2,1)} %broadcast_in_dim.30, s32[40]{0:T(128)S(1)} %fusion.17, bf16[40,128,512]{2,1,0:T(8,128)(2,1)} %broadcast_select_fusion), kind=kCustom, calls=%fused_computation.5 | custom fusion | bytes 15728800 | tf_op jit(solution)/shard_map/scatter | solution.py:29
  180.7 0.0 all-to-all-done
  180.7 11.0 %all-to-all-start.1 = ((bf16[64,1,128,512]{3,2,1,0:T(8,128)(2,1)}), bf16[64,1,128,512]{3,2,1,0:T(8,128)(2,1)}, u32[]{:S(2)}, u32[]{:S(2)}) async-start(bf16[64,1,128,512]{3,2,1,0:T(8,128)(2,1)} %bitcast.36), calls=%async_computation.1 | async-start | bytes 16777216 | tf_op jit(solution)/shard_map/all_to_all | solution.py:68
  191.7 0.0 copy-start
  191.7 1.2 reduce
  193.0 184.5 %all-to-all-done.1 = bf16[64,1,128,512]{3,2,1,0:T(8,128)(2,1)} async-done(((bf16[64,1,128,512]{3,2,1,0:T(8,128)(2,1)}), bf16[64,1,128,512]{3,2,1,0:T(8,128)(2,1)}, u32[]{:S(2)}, u32[]{:S(2)}) %all-to-all-start.1) | async-done | bytes 8388640 | tf_op jit(solution)/shard_map/all_to_all | solution.py:68
  377.5 12.3 %fusion.4 = f32[4,128,512]{2,0,1:T(4,128)S(1)} fusion(bf16[64,1,128,512]{3,2,1,0:T(8,128)(2,1)} %all-to-all-done.1, s32[64]{0:T(128)S(1)} %reduce), kind=kOutput, calls=%fused_computation.12 | convolution fusion | flops 33554688 | bytes 9437440 | tf_op jit(solution)/shard_map/tn,nrc->trc/dot_general | solution.py:40
  389.7 0.0 copy-done
  389.7 1.4 copy_subtract_fusion
  (5 shorter events, 0.0 us)
Async XLA Ops:
  6.5 24.6 %copy-start.1 = (s32[10]{0:T(128)S(1)}, s32[10]{0:T(128)}, u32[]{:S(2)}) copy-start(s32[10]{0:T(128)} %constant.35) | copy-start | bytes 124
  6.5 24.6 %copy-start.2 = (s32[1,40]{1,0:T(1,128)S(1)}, s32[1,40]{1,0:T(1,128)}, u32[]{:S(2)}) copy-start(s32[1,40]{1,0:T(1,128)} %param.12) | copy-start | bytes 484
  6.5 91.9 %all-gather.3.cloned.1.call-start = ((), (), s32[]{:S(2)}) async-start(), calls=%async_computation.2 | async-start | bytes 10485760 | tf_op jit(solution)/shard_map/all_gather | solution.py:64
  11.1 169.6 %all-to-all-start = ((s32[64,1,1]{2,1,0:T(1,128)}), s32[64,1,1]{2,1,0:T(1,128)S(1)}, u32[]{:S(2)}, u32[]{:S(2)}) async-start(s32[64,1,1]{2,1,0:T(1,128)} %copy.45), calls=%async_computation | async-start | bytes 65536 | tf_op jit(solution)/shard_map/all_to_all | solution.py:69
  119.5 20.0 %slice-start = ((s8[5242880]{0:T(1024)(128)(4,1)}), s8[1048576]{0:T(1024)(128)(4,1)S(1)}, s32[]{:S(2)}) async-start(s8[5242880]{0:T(1024)(128)(4,1)} %bitcast.39), calls=%async_computation.3 | async-start | bytes 2097152
  127.1 12.4 %slice-start.1 = ((s8[5242880]{0:T(1024)(128)(4,1)}), s8[4194304]{0:T(1024)(128)(4,1)S(1)}, s32[]{:S(2)}) async-start(s8[5242880]{0:T(1024)(128)(4,1)} %bitcast.39), calls=%async_computation.4 | async-start | bytes 8388608
  180.7 196.7 %all-to-all-start.1 = ((bf16[64,1,128,512]{3,2,1,0:T(8,128)(2,1)}), bf16[64,1,128,512]{3,2,1,0:T(8,128)(2,1)}, u32[]{:S(2)}, u32[]{:S(2)}) async-start(bf16[64,1,128,512]{3,2,1,0:T(8,128)(2,1)} %bitcast.36), calls=%async_computation.1 | async-start | bytes 16777216 | tf_op jit(solution)/shard_map/all_to_all | solution.py:68
  191.7 198.0 %copy-start = (f32[4,128,512]{2,1,0:T(8,128)S(1)}, f32[4,128,512]{2,1,0:T(8,128)}, u32[]{:S(2)}) copy-start(f32[4,128,512]{2,1,0:T(8,128)} %param.11) | copy-start | bytes 3145732
Sparse Core Ops, SparseCore 0:
  9.1 89.2 all-gather.2
